TPU v7x, 32 devices: a whole 2x2x4 slice. The times are simulated.
32 devices in a mesh: beam: 2 (over y), tm: 4 (over z), sect: 2 (over x), pol: 2 (over core).
Axes of the slice: x: 2, y: 2, z: 4, core: 2. Of those that a mesh axis runs over, the one named last changes fastest.
Arguments:
- signal: float32 [2, 2, 512, 4096], P(None, 'pol', ('beam', 'tm', 'sect')), parts along dimension 2, may hold values from -6 to 6
- coarse_taps: float32 [16, 4096], replicated, may hold values from -1.5 to 1.5
- fine_taps: float32 [16, 1024], replicated, may hold values from -1.5 to 1.5
- channel_order: int32 [4096], replicated, may hold values from 0 to 4095, each once
Outputs:
- fine_spectra: float32 [2, 2, 8192, 1, 1024], P(None, 'pol', ('beam', 'tm', 'sect')), parts along dimension 2
There are 2 independent parts, one for each index of `beam`. A program takes and returns all parts, laid end to end along the dimension named above; an argument that names none is the same for every part. Nothing has to cross between parts.
Inputs may be any that keep to these rules, and one draw needn't show every extreme that they name: `channel_order`: each of the 4096 coarse channels appears exactly once.
All inputs are finite; a program needn't handle non-finite values.
Results may differ from a plain program's by a relative error of at most 0.0001.
Values sent between devices are 32-bit elements; how exact they have to be, the bound alone decides.
No kernel may reach another device: no remote copies, remote signals or barrier semaphores. Data moves between devices by JAX's collectives and lax.ppermute only.
A program may use at most 128 MiB of HBM per device.

v0:
```python
from functools import partial
import math

import jax
import jax.numpy as jnp
import numpy as np
from jax import lax
from jax.experimental import pallas as pl
from jax.experimental.pallas import tpu as pltpu
from jax.sharding import PartitionSpec as P


LANES = 128
ROWS = 8
HALF = 16
SIDES = LANES // (2 * HALF)


def split(value):
    high = value.astype(jnp.bfloat16)
    return high, (value - high.astype(jnp.float32)).astype(jnp.bfloat16)


def host_split(value):
    high = value.astype(jnp.bfloat16)
    return high, (value - high.astype(np.float32)).astype(jnp.bfloat16)


def dft(rows, cols, period):
    angles = np.outer(np.arange(rows), np.arange(cols)) % period * (-2.0 * np.pi / period)
    return np.cos(angles), np.sin(angles)


def product3(left, right, dims):
    dot = partial(
        lax.dot_general, dimension_numbers=(dims, ((), ())), preferred_element_type=jnp.float32
    )
    return dot(left[0], right[0]) + (dot(left[0], right[1]) + dot(left[1], right[0]))


def coarse_tables(width):
    count = width // LANES
    re, im = dft(count, count, count)
    first = np.kron(np.block([[re, -im], [im, re]]), np.eye(ROWS)).astype(np.float32)
    twist = np.stack(dft(count, LANES, width)).astype(np.float32)
    re, im = dft(LANES, LANES, LANES)
    second = (np.concatenate([re, im], axis=1) / math.sqrt(width)).astype(np.float32)
    return (*host_split(first), twist, *host_split(second))


def coarse_kernel(first, index_ref, signal_ref, *refs):
    *next_refs, taps_ref, first_hi, first_lo, twist_ref, second_hi, second_lo = refs[:-7]
    out_ref, ext_ref, in_hi, in_lo, mid_hi, mid_lo, spec_ref = refs[-7:]
    next_ref, start = (next_refs[0], 0) if next_refs else (signal_ref, first + HALF)
    slab, width = HALF, signal_ref.shape[2]
    tap_count = taps_ref.shape[0]
    lead = tap_count - 1
    count = width // LANES
    groups = slab // ROWS
    for part in range(2):
        for a in range(count):
            cols = slice(a * LANES, (a + 1) * LANES)
            ext_ref[part, a, 0:slab] = signal_ref[part, first : first + slab, cols]
            ext_ref[part, a, slab : slab + lead] = next_ref[part, start : start + lead, cols]

    def filter_pair(pair, carry):
        tiles = []
        for half in range(2):
            a = 2 * pair + half
            taps = taps_ref[:, pl.ds(pl.multiple_of(a * LANES, LANES), LANES)]
            for part in range(2):
                for group in range(groups):
                    total = taps[0:1] * ext_ref[part, a, group * ROWS : (group + 1) * ROWS]
                    for k in range(1, tap_count):
                        row = group * ROWS + k
                        total = total + taps[k : k + 1] * ext_ref[part, a, row : row + ROWS]
                    tiles.append(total)
        for part in range(2):
            for group in range(groups):
                both = jnp.concatenate(
                    [tiles[part * groups + group], tiles[(2 + part) * groups + group]], axis=0
                )
                high, low = split(both)
                row = pl.multiple_of(part * count * ROWS + pair * 2 * ROWS, 2 * ROWS)
                in_hi[pl.ds(row, 2 * ROWS), group * LANES : (group + 1) * LANES] = high
                in_lo[pl.ds(row, 2 * ROWS), group * LANES : (group + 1) * LANES] = low
        return carry

    lax.fori_loop(0, count // 2, filter_pair, 0)

    inputs = (in_hi[...], in_lo[...])
    step = 8
    for chunk in range(count // step):
        rows = [
            slice((part * count + chunk * step) * ROWS, (part * count + (chunk + 1) * step) * ROWS)
            for part in range(2)
        ]
        re, im = [
            product3((first_hi[r, :], first_lo[r, :]), inputs, ((1,), (0,))) for r in rows
        ]
        twist_re = twist_ref[0, chunk * step : (chunk + 1) * step][:, None, :]
        twist_im = twist_ref[1, chunk * step : (chunk + 1) * step][:, None, :]
        turned_re, turned_im = [], []
        for group in range(groups):
            cols = slice(group * LANES, (group + 1) * LANES)
            sec_re = re[:, cols].reshape(step, ROWS, LANES)
            sec_im = im[:, cols].reshape(step, ROWS, LANES)
            turned_re.append(sec_re * twist_re - sec_im * twist_im)
            turned_im.append(sec_re * twist_im + sec_im * twist_re)
        turned_re = jnp.concatenate(turned_re, axis=1)
        turned_im = jnp.concatenate(turned_im, axis=1)
        upper = jnp.concatenate([turned_re, -turned_im], axis=2)
        lower = jnp.concatenate([turned_im, turned_re], axis=2)
        both = jnp.concatenate([upper, lower], axis=1).reshape(step * 2 * slab, 2 * LANES)
        high, low = split(both)
        mid_hi[chunk * step * 2 * slab : (chunk + 1) * step * 2 * slab, :] = high
        mid_lo[chunk * step * 2 * slab : (chunk + 1) * step * 2 * slab, :] = low

    tiles = count // SIDES
    for tile in range(tiles // 2):
        rows = slice(tile * 2 * LANES, (tile + 1) * 2 * LANES)
        both = product3(
            (second_hi[...], second_lo[...]), (mid_hi[rows, :], mid_lo[rows, :]), ((1,), (1,))
        )
        for sub in range(2):
            spec = both[:, sub * LANES : (sub + 1) * LANES]
            for turn in range(SIDES):
                base = (turn * tiles + 2 * tile + sub) * LANES
                rolled = pltpu.roll(spec, turn * 2 * HALF, 1) if turn else spec
                spec_ref[base : base + LANES, :] = rolled

    total = out_ref.shape[0]
    lane = lax.broadcasted_iota(jnp.int32, (1, LANES), 1)

    def gather(block, carry):
        for row in range(ROWS):
            q = block * ROWS + row
            got = [spec_ref[pl.ds(index_ref[side * total + q], 1), :] for side in range(SIDES)]
            value = got[-1]
            for side in range(SIDES - 2, -1, -1):
                value = jnp.where(lane < (side + 1) * 2 * HALF, got[side], value)
            out_ref[pl.ds(q, 1), :] = value
        return carry

    lax.fori_loop(0, total // ROWS, gather, 0)


def slot_rows(channel_order, width, owners):
    count = width // LANES
    order = channel_order.reshape(owners, SIDES, width // owners // SIDES).swapaxes(0, 1)
    k, m = order % count, order // count
    turn = (jnp.arange(SIDES, dtype=jnp.int32)[:, None, None] - k % SIDES) % SIDES
    return ((turn * (count // SIDES) + k // SIDES) * LANES + m).reshape(width)


def coarse_bank(first, signals, taps, index):
    width = taps.shape[1]
    count = width // LANES
    vmem = pl.BlockSpec(memory_space=pltpu.VMEM)
    size = 2 * count * ROWS
    groups = HALF // ROWS
    return pl.pallas_call(
        partial(coarse_kernel, first),
        out_shape=jax.ShapeDtypeStruct((width // SIDES, LANES), jnp.float32),
        in_specs=[pl.BlockSpec(memory_space=pltpu.SMEM)] + [vmem] * (len(signals) + 6),
        out_specs=vmem,
        scratch_shapes=[
            pltpu.VMEM((2, count, HALF + 16, LANES), jnp.float32),
            pltpu.VMEM((size, groups * LANES), jnp.bfloat16),
            pltpu.VMEM((size, groups * LANES), jnp.bfloat16),
            pltpu.VMEM((count * 2 * HALF, 2 * LANES), jnp.bfloat16),
            pltpu.VMEM((count * 2 * HALF, 2 * LANES), jnp.bfloat16),
            pltpu.VMEM((count * LANES, LANES), jnp.float32),
        ],
    )(index, *signals, taps, *coarse_tables(width))


def table_kernel(base_ref, turn_ref, high_ref, low_ref):
    length = base_ref.shape[1]
    width = high_ref.shape[1] // 2
    slab = HALF
    for c in range(width // LANES):
        turn_re, turn_im = turn_ref[0, :, c : c + 1], turn_ref[1, :, c : c + 1]
        re = base_ref[0] * turn_re - base_ref[1] * turn_im
        im = base_ref[0] * turn_im + base_ref[1] * turn_re
        re, im = [value.reshape(length // slab, 1, slab, LANES) for value in (re, im)]
        for part, value in enumerate((jnp.concatenate([re, -im], 1), jnp.concatenate([im, re], 1))):
            high, low = split(value.reshape(2 * length, LANES))
            cols = slice(part * width + c * LANES, part * width + (c + 1) * LANES)
            high_ref[:, cols] = high
            low_ref[:, cols] = low


def by_half(value, axis, parts):
    shape = value.shape
    value = value.reshape(*shape[:axis], -1, parts, HALF, *shape[axis + 1 :])
    return value.swapaxes(axis, axis + 1).reshape(shape)


def fine_tables(length, width, parts):
    base = by_half(np.stack(dft(length, LANES, width)).astype(np.float32), 1, parts)
    turn = np.stack(dft(length, width // LANES, width // LANES)).astype(np.float32)
    turn = by_half(turn, 1, parts)
    vmem = pl.BlockSpec(memory_space=pltpu.VMEM)
    shape = jax.ShapeDtypeStruct((2 * length, 2 * width), jnp.bfloat16)
    return pl.pallas_call(
        table_kernel, out_shape=(shape, shape), in_specs=[vmem] * 2, out_specs=(vmem, vmem),
        name="table",
    )(base, turn)


def fine_kernel(taps_ref, *refs):
    *arrived, high_ref, low_ref, out_ref = refs
    sources, rows = arrived[0].shape[:2]
    width = high_ref.shape[1] // 2
    count = width // LANES
    piece = 2 * HALF
    x = jnp.concatenate(
        [
            jnp.concatenate(
                [
                    ref[s, :, side * piece : (side + 1) * piece]
                    for ref in arrived
                    for s in range(sources)
                ],
                axis=1,
            )
            for side in range(SIDES)
        ],
        axis=0,
    )
    x = split(x * taps_ref[...])
    for col in range(count):
        cols = slice(col * 2 * LANES, (col + 1) * 2 * LANES)
        y = product3(x, (high_ref[:, cols], low_ref[:, cols]), ((1,), (0,)))
        for sub in range(2):
            part, c = divmod(2 * col + sub, count)
            for side in range(SIDES):
                out_ref[part, side, pl.ds(c, rows, stride=count), :] = y[
                    side * rows : (side + 1) * rows, sub * LANES : (sub + 1) * LANES
                ]


def short_fine_bank(fine_taps, arrived, tables):
    parts = len(arrived)
    sources, own_rows = arrived[0].shape[:2]
    width = fine_taps.shape[1]
    length = parts * sources * HALF
    taps = by_half(fine_taps[0, :length] * (1.0 / math.sqrt(width)), 0, parts)
    taps = jnp.broadcast_to(taps.reshape(-1, 1, HALF), (parts * sources, 2, HALF))
    taps = taps.reshape(1, 2 * length)
    steps = 2
    block = own_rows // steps
    count = width // LANES
    full = lambda shape: pl.BlockSpec(shape, lambda i: (0, 0))
    out = pl.pallas_call(
        fine_kernel,
        grid=(steps,),
        out_shape=jax.ShapeDtypeStruct((2, SIDES, own_rows * count, LANES), jnp.float32),
        in_specs=[full((1, 2 * length))]
        + [pl.BlockSpec((sources, block, LANES), lambda i: (0, i, 0))] * parts
        + [full((2 * length, 2 * width))] * 2,
        out_specs=pl.BlockSpec((2, SIDES, block * count, LANES), lambda i: (0, 0, i, 0)),
        name="fine",
    )(taps, *arrived, *tables)
    return out.reshape(2, 1, SIDES * own_rows, 1, width)


def shifted(value, axis, steps):
    count = lax.axis_size(axis)
    initial, last = (max(0, -steps), min(count, count - steps))
    return lax.ppermute(value, axis, [(source, source + steps) for source in range(initial, last)])


def complex_einsum(form, left_re, left_im, right_re, right_im):
    product = partial(jnp.einsum, form, precision=lax.Precision.HIGH)
    return (
        product(left_re, right_re) - product(left_im, right_im),
        product(left_re, right_im) + product(left_im, right_re),
    )


def fine_table(rows, width):
    samples = np.arange(rows)[:, None] * np.arange(width)[None, :] % width
    angles = samples * (-2.0 * np.pi / width)
    return np.cos(angles).astype(np.float32), np.sin(angles).astype(np.float32)


def fine_bank(fine_taps, series):
    total_len = series.shape[3]
    tap_count, fine_width = fine_taps.shape
    frames = -(-total_len // fine_width)
    length = min(total_len, fine_width)
    padded = jnp.pad(series, ((0, 0), (0, 0), (0, 0), (0, frames * length - total_len)))
    blocks = padded.reshape(*series.shape[:3], frames, length)
    rows = []
    for frame in range(frames):
        row = fine_taps[0, :length] * blocks[:, :, :, frame]
        for tap_index in range(1, min(tap_count, frames - frame)):
            row = row + fine_taps[tap_index, :length] * blocks[:, :, :, frame + tap_index]
        rows.append(row)
    filtered = jnp.stack(rows, axis=3) * (1.0 / math.sqrt(fine_width))
    table_re, table_im = fine_table(length, fine_width)
    out_re, out_im = complex_einsum("pnfj,jm->pnfm", filtered[0], filtered[1], table_re, table_im)
    return jnp.stack([out_re, out_im])


def bank(signal, coarse_taps, fine_taps, channel_order):
    slab_len, width = signal.shape[2:]
    lead = coarse_taps.shape[0] - 1
    assert slab_len % HALF == 0 and lead <= HALF
    signal = signal[:, 0]
    next_rows = shifted(signal[:, :lead], ("tm", "sect"), -1)
    owners = lax.axis_size(("tm", "sect"))
    own = width // owners
    length = owners * slab_len
    parts = slab_len // HALF
    short = length <= fine_taps.shape[1]
    index = slot_rows(channel_order, width, owners)
    arrived = []
    for part in range(parts):
        first = part * HALF
        signals = [signal] if part < parts - 1 else [signal, next_rows]
        ordered = coarse_bank(first, signals, coarse_taps, index)
        blocks = ordered.reshape(owners, own // SIDES, LANES)
        arrived.append(
            lax.all_to_all(blocks, ("tm", "sect"), split_axis=0, concat_axis=0, tiled=True)
        )
    if short:
        tables = fine_tables(length, fine_taps.shape[1], parts)
        return short_fine_bank(fine_taps, arrived, tables)
    series = jnp.stack(arrived).reshape(parts, owners, own // SIDES, SIDES, 2, HALF)
    series = series.transpose(4, 3, 2, 1, 0, 5)
    return fine_bank(fine_taps, series.reshape(2, 1, own, length))


def solution(mesh):
    in_specs = (P(None, "pol", ("beam", "tm", "sect"), None), P(), P(), P())
    out_specs = P(None, "pol", ("beam", "tm", "sect"), None, None)
    return jax.shard_map(bank, mesh=mesh, in_specs=in_specs, out_specs=out_specs, check_vma=False)
```

profile of v0, /device:TPU:0, one launch (start us, length us, event | category | flops | bytes accessed | tf_op | source)
XLA Modules:
  0.0 79.2 jit_solution(18351881096528685456)
XLA Ops:
  0.0 0.0 copy-start
  0.0 0.9 %fusion.5 = s32[4,8,128]{2,0,1:T(4,128)S(1)} fusion(s32[4,8,128]{2,0,1:T(4,128)} %bitcast.23), kind=kLoop, calls=%fused_computation.18 | loop fusion | flops 221184 | bytes 32768 | tf_op jit(solution)/shard_map/add | solution.py:153
  0.9 0.6 copy.24
  1.5 9.3 %shard_map.154 = f32[1024,128]{1,0:T(8,128)} custom-call(s32[4096]{0:T(1024)} %bitcast.19, f32[2,32,4096]{2,1,0:T(8,128)} %bitcast.14, f32[16,4096]{1,0:T(8,128)} %refs_1_.2, bf16[512,512]{1,0:T(8,128)(2,1)} %constant.73.clone.refs_1_.refs_2_, bf16[512,512]{1,0:T(8,128)(2,1)} %constant.74.clone.refs_2_.refs_3_, ...), custom_call_target="tpu_custom_call" | custom-call | tf_op jit(solution)/shard_map/pallas_call | solution.py:162
  10.8 7.3 %all-to-all-start = ((f32[8,128,128]{2,1,0:T(8,128)}), f32[8,128,128]{2,1,0:T(8,128)S(1)}, u32[]{:S(2)}, u32[]{:S(2)}) async-start(f32[8,128,128]{2,1,0:T(8,128)} %bitcast.18), calls=%async_computation | async-start | bytes 1048576 | tf_op jit(solution)/shard_map/all_to_all | solution.py:327
  18.1 0.0 copy-done
  18.2 1.3 %collective-permute-start = (f32[2,15,4096]{2,1,0:T(8,128)S(1)}, f32[2,15,4096]{2,1,0:T(8,128)S(1)}, u32[]{:S(2)}, u32[]{:S(2)}) collective-permute-start(f32[2,15,4096]{2,1,0:T(8,128)S(1)} %slice.8), channel_id=1, source_target_pairs={{2,0},{4,2},{6,4},{8,6},{10,8},{12,10},{14,12},{3,1},{5,3},{7,5},{... | collective-permute-start | bytes 1474568 | tf_op jit(solution)/shard_map/ppermute | solution.py:272
  19.5 18.6 %collective-permute-done.refs_0_ = f32[2,15,4096]{2,1,0:T(8,128)S(1)} collective-permute-done((f32[2,15,4096]{2,1,0:T(8,128)S(1)}, f32[2,15,4096]{2,1,0:T(8,128)S(1)}, u32[]{:S(2)}, u32[]{:S(2)}) %collective-permute-start) | collective-permute-done | bytes 491552 | tf_op jit(solution)/shard_map/ppermute | solution.py:272
  38.0 0.0 copy-start.3
  38.0 0.8 copy-done.3
  38.8 9.5 %shard_map.155 = f32[1024,128]{1,0:T(8,128)} custom-call(s32[4096]{0:T(1024)} %bitcast.20, f32[2,32,4096]{2,1,0:T(8,128)} %bitcast.15, f32[2,15,4096]{2,1,0:T(8,128)} %copy-done.3, f32[16,4096]{1,0:T(8,128)} %refs_1_.2, bf16[512,512]{1,0:T(8,128)(2,1)} %constant.73.clone.refs_1_.refs_2_, bf16[512,512]{1,0:T(8,128)(2,1)} %constant.74.clone.refs_2_.refs_3_, ...), custom_call_target="tpu_custom_call" | custom-call | tf_op jit(solution)/shard_map/pallas_call | solution.py:162
  48.3 0.0 all-to-all-done.refs_0_
  48.3 0.0 copy-start.1
  48.3 8.5 %all-to-all-start.1 = ((f32[8,128,128]{2,1,0:T(8,128)}), f32[8,128,128]{2,1,0:T(8,128)S(1)}, u32[]{:S(2)}, u32[]{:S(2)}) async-start(f32[8,128,128]{2,1,0:T(8,128)} %bitcast.17), calls=%async_computation.1 | async-start | bytes 1048576 | tf_op jit(solution)/shard_map/all_to_all | solution.py:327
  56.9 0.7 multiply_reduce_fusion
  57.6 0.1 mul.24
  57.7 0.7 reshape.23.taps_ref
  58.4 4.4 %table.1 = (bf16[512,2048]{1,0:T(8,128)(2,1)}, bf16[512,2048]{1,0:T(8,128)(2,1)}) custom-call(f32[2,256,128]{2,1,0:T(8,128)} %constant.78.clone.base_ref, f32[2,256,8]{2,1,0:T(8,128)} %constant.79.clone.turn_ref), custom_call_target="tpu_custom_call" | custom-call | tf_op jit(solution)/shard_map/table/pallas_call | solution.py:206
  62.7 7.5 %all-to-all-done.1.refs_1_ = f32[8,128,128]{2,1,0:T(8,128)S(1)} async-done(((f32[8,128,128]{2,1,0:T(8,128)}), f32[8,128,128]{2,1,0:T(8,128)S(1)}, u32[]{:S(2)}, u32[]{:S(2)}) %all-to-all-start.1) | async-done | bytes 524320 | tf_op jit(solution)/shard_map/all_to_all | solution.py:327
  70.2 0.0 copy-start.2
  70.2 0.0 copy-done.1
  70.2 0.8 %copy-done.2 = f32[8,128,128]{2,1,0:T(8,128)} copy-done((f32[8,128,128]{2,1,0:T(8,128)}, f32[8,128,128]{2,1,0:T(8,128)S(1)}, u32[]{:S(2)}) %copy-start.2) | copy-done | bytes 524312
  71.0 8.2 %fine.1 = f32[2,4,1024,128]{3,2,1,0:T(8,128)} custom-call(f32[1,512]{1,0:T(1,128)} %reshape.23.taps_ref, f32[8,128,128]{2,1,0:T(8,128)} %copy-done.1, f32[8,128,128]{2,1,0:T(8,128)} %copy-done.2, bf16[512,2048]{1,0:T(8,128)(2,1)} %get-tuple-element.7.refs_2_, bf16[512,2048]{1,0:T(8,128)(2,1)} %get-tuple-element.8.refs_3_), custom_call_target="tpu_custom_call" | custom-call | tf_op jit(solution)/shard_map/fine/pallas_call | solution.py:256
  (3 shorter events, 0.0 us)
Async XLA Ops:
  0.0 18.1 %copy-start = (f32[2,1,32,4096]{3,2,1,0:T(8,128)S(1)}, f32[2,1,32,4096]{3,2,1,0:T(8,128)}, u32[]{:S(2)}) copy-start(f32[2,1,32,4096]{3,2,1,0:T(8,128)} %param.16) | copy-start | bytes 3145732
  10.8 37.5 %all-to-all-start = ((f32[8,128,128]{2,1,0:T(8,128)}), f32[8,128,128]{2,1,0:T(8,128)S(1)}, u32[]{:S(2)}, u32[]{:S(2)}) async-start(f32[8,128,128]{2,1,0:T(8,128)} %bitcast.18), calls=%async_computation | async-start | bytes 1048576 | tf_op jit(solution)/shard_map/all_to_all | solution.py:327
  18.2 19.9 %collective-permute-start = (f32[2,15,4096]{2,1,0:T(8,128)S(1)}, f32[2,15,4096]{2,1,0:T(8,128)S(1)}, u32[]{:S(2)}, u32[]{:S(2)}) collective-permute-start(f32[2,15,4096]{2,1,0:T(8,128)S(1)} %slice.8), channel_id=1, source_target_pairs={{2,0},{4,2},{6,4},{8,6},{10,8},{12,10},{14,12},{3,1},{5,3},{7,5},{... | collective-permute-start | bytes 1474568 | tf_op jit(solution)/shard_map/ppermute | solution.py:272
  38.0 0.8 copy-start.3
  48.3 21.9 %copy-start.1 = (f32[8,128,128]{2,1,0:T(8,128)}, f32[8,128,128]{2,1,0:T(8,128)S(1)}, u32[]{:S(2)}) copy-start(f32[8,128,128]{2,1,0:T(8,128)S(1)} %all-to-all-done.refs_0_) | copy-start | bytes 1572868
  48.3 21.9 %all-to-all-start.1 = ((f32[8,128,128]{2,1,0:T(8,128)}), f32[8,128,128]{2,1,0:T(8,128)S(1)}, u32[]{:S(2)}, u32[]{:S(2)}) async-start(f32[8,128,128]{2,1,0:T(8,128)} %bitcast.17), calls=%async_computation.1 | async-start | bytes 1048576 | tf_op jit(solution)/shard_map/all_to_all | solution.py:327
  70.2 0.8 %copy-start.2 = (f32[8,128,128]{2,1,0:T(8,128)}, f32[8,128,128]{2,1,0:T(8,128)S(1)}, u32[]{:S(2)}) copy-start(f32[8,128,128]{2,1,0:T(8,128)S(1)} %all-to-all-done.1.refs_1_) | copy-start | bytes 1572868
where the time goes:
time: 79.6 us; the launch traced here: 79.2 us
  Pallas kernels  31.3 us (39%)
  waiting for transfers between devices  26.1 us (33%)
  starting transfers between devices  17.1 us (21%)
  local copies, waits for them, and re-layouts  3.01 us (4%)
  other arithmetic  1.6 us (2%)
    pallas_call x2, Pallas kernels, coarse_bank(): pl.pallas_call(partial(coarse_kernel, first), out_shape=jax.ShapeDtypeStr...  18.8 us
    ppermute x1, waiting for transfers between devices, shifted(): lax.ppermute(value, axis, [(source, source + steps) for source in range(i...  18.6 us
    all_to_all x2, starting transfers between devices, bank(): lax.all_to_all(blocks, ('tm', 'sect'), split_axis=0, concat_axis=0, tiled...  15.8 us
    pallas_call x1, Pallas kernels, short_fine_bank(): pl.pallas_call(fine_kernel, grid=(steps,), out_shape=jax.ShapeDtypeStruct...  8.18 us
    all_to_all x2, waiting for transfers between devices, bank(): lax.all_to_all(blocks, ('tm', 'sect'), split_axis=0, concat_axis=0, tiled...  7.48 us
    pallas_call x1, Pallas kernels, fine_tables(): pl.pallas_call(table_kernel, out_shape=(shape, shape), in_specs=[vmem] *...  4.35 us
    unnamed x8, local copies, waits for them, and re-layouts  1.59 us
  transfers between devices with their start and end apart: 3, of which 2 were waited for; matrix products, arithmetic and copies ran while one was open for 2% of the time, Pallas kernels for 17%

commit v1 on v0

--- a/solution.py
+++ b/solution.py
@@ -35,7 +35,9 @@
     dot = partial(
         lax.dot_general, dimension_numbers=(dims, ((), ())), preferred_element_type=jnp.float32
     )
-    return dot(left[0], right[0]) + (dot(left[0], right[1]) + dot(left[1], right[0]))
+    rows = left[0].shape[0]
+    both = dot(jnp.concatenate(left, axis=0), right[0])
+    return both[:rows] + (both[rows:] + dot(left[0], right[1]))
 
 
 def coarse_tables(width):
@@ -132,17 +134,24 @@
     total = out_ref.shape[0]
     lane = lax.broadcasted_iota(jnp.int32, (1, LANES), 1)
 
+    batch = math.gcd(total, 32)
+
     def gather(block, carry):
-        for row in range(ROWS):
-            q = block * ROWS + row
+        values = []
+        for row in range(batch):
+            q = block * batch + row
             got = [spec_ref[pl.ds(index_ref[side * total + q], 1), :] for side in range(SIDES)]
             value = got[-1]
             for side in range(SIDES - 2, -1, -1):
                 value = jnp.where(lane < (side + 1) * 2 * HALF, got[side], value)
-            out_ref[pl.ds(q, 1), :] = value
+            values.append(value)
+        for tile in range(batch // ROWS):
+            out_ref[pl.ds(pl.multiple_of(block * batch + tile * ROWS, ROWS), ROWS), :] = (
+                jnp.concatenate(values[tile * ROWS : (tile + 1) * ROWS], axis=0)
+            )
         return carry
 
-    lax.fori_loop(0, total // ROWS, gather, 0)
+    lax.fori_loop(0, total // batch, gather, 0)
 
 
 def slot_rows(channel_order, width, owners):

time: 79.6 us -> 77.7 us (0.976)
  Pallas kernels: 31.3 us -> 29.4 us
    pallas_call x2, Pallas kernels: 18.8 us -> 16.9 us  [coarse_bank(): pl.pallas_call(partial(coarse_kernel, first), out_shape=jax.ShapeDtypeStr...]
where the time goes in v1:
time: 77.7 us; the launch traced here: 77.2 us
  Pallas kernels  29.4 us (38%)
  waiting for transfers between devices  26.1 us (34%)
  starting transfers between devices  17.1 us (22%)
  local copies, waits for them, and re-layouts  3.01 us (4%)
  other arithmetic  1.6 us (2%)
    ppermute x1, waiting for transfers between devices, shifted(): lax.ppermute(value, axis, [(source, source + steps) for source in range(i...  18.6 us
    pallas_call x2, Pallas kernels, coarse_bank(): pl.pallas_call(partial(coarse_kernel, first), out_shape=jax.ShapeDtypeStr...  16.9 us
    all_to_all x2, starting transfers between devices, bank(): lax.all_to_all(blocks, ('tm', 'sect'), split_axis=0, concat_axis=0, tiled...  15.8 us
    pallas_call x1, Pallas kernels, short_fine_bank(): pl.pallas_call(fine_kernel, grid=(steps,), out_shape=jax.ShapeDtypeStruct...  8.09 us
    all_to_all x2, waiting for transfers between devices, bank(): lax.all_to_all(blocks, ('tm', 'sect'), split_axis=0, concat_axis=0, tiled...  7.49 us
    pallas_call x1, Pallas kernels, fine_tables(): pl.pallas_call(table_kernel, out_shape=(shape, shape), in_specs=[vmem] *...  4.35 us
    unnamed x8, local copies, waits for them, and re-layouts  1.59 us
  transfers between devices with their start and end apart: 3, of which 2 were waited for; matrix products, arithmetic and copies ran while one was open for 2% of the time, Pallas kernels for 17%

profile of v1, /device:TPU:0, one launch (start us, length us, event | category | flops | bytes accessed | tf_op | source)
XLA Modules:
  0.0 77.2 jit_solution(814706976170485164)
XLA Ops:
  0.0 0.0 copy-start
  0.0 0.9 %fusion.5 = s32[4,8,128]{2,0,1:T(4,128)S(1)} fusion(s32[4,8,128]{2,0,1:T(4,128)} %bitcast.23), kind=kLoop, calls=%fused_computation.18 | loop fusion | flops 221184 | bytes 32768 | tf_op jit(solution)/shard_map/add | solution.py:162
  0.9 0.6 copy.24
  1.5 8.4 %shard_map.154 = f32[1024,128]{1,0:T(8,128)} custom-call(s32[4096]{0:T(1024)} %bitcast.19, f32[2,32,4096]{2,1,0:T(8,128)} %bitcast.14, f32[16,4096]{1,0:T(8,128)} %refs_1_.2, bf16[512,512]{1,0:T(8,128)(2,1)} %constant.73.clone.refs_1_.refs_2_, bf16[512,512]{1,0:T(8,128)(2,1)} %constant.74.clone.refs_2_.refs_3_, ...), custom_call_target="tpu_custom_call" | custom-call | tf_op jit(solution)/shard_map/pallas_call | solution.py:171
  9.9 7.3 %all-to-all-start = ((f32[8,128,128]{2,1,0:T(8,128)}), f32[8,128,128]{2,1,0:T(8,128)S(1)}, u32[]{:S(2)}, u32[]{:S(2)}) async-start(f32[8,128,128]{2,1,0:T(8,128)} %bitcast.18), calls=%async_computation | async-start | bytes 1048576 | tf_op jit(solution)/shard_map/all_to_all | solution.py:336
  17.1 0.0 copy-done
  17.2 1.3 %collective-permute-start = (f32[2,15,4096]{2,1,0:T(8,128)S(1)}, f32[2,15,4096]{2,1,0:T(8,128)S(1)}, u32[]{:S(2)}, u32[]{:S(2)}) collective-permute-start(f32[2,15,4096]{2,1,0:T(8,128)S(1)} %slice.8), channel_id=1, source_target_pairs={{2,0},{4,2},{6,4},{8,6},{10,8},{12,10},{14,12},{3,1},{5,3},{7,5},{... | collective-permute-start | bytes 1474568 | tf_op jit(solution)/shard_map/ppermute | solution.py:281
  18.5 18.6 %collective-permute-done.refs_0_ = f32[2,15,4096]{2,1,0:T(8,128)S(1)} collective-permute-done((f32[2,15,4096]{2,1,0:T(8,128)S(1)}, f32[2,15,4096]{2,1,0:T(8,128)S(1)}, u32[]{:S(2)}, u32[]{:S(2)}) %collective-permute-start) | collective-permute-done | bytes 491552 | tf_op jit(solution)/shard_map/ppermute | solution.py:281
  37.1 0.0 copy-start.3
  37.1 0.8 %copy-done.3 = f32[2,15,4096]{2,1,0:T(8,128)} copy-done((f32[2,15,4096]{2,1,0:T(8,128)}, f32[2,15,4096]{2,1,0:T(8,128)S(1)}, u32[]{:S(2)}) %copy-start.3) | copy-done | bytes 491544
  37.9 8.5 %shard_map.155 = f32[1024,128]{1,0:T(8,128)} custom-call(s32[4096]{0:T(1024)} %bitcast.20, f32[2,32,4096]{2,1,0:T(8,128)} %bitcast.15, f32[2,15,4096]{2,1,0:T(8,128)} %copy-done.3, f32[16,4096]{1,0:T(8,128)} %refs_1_.2, bf16[512,512]{1,0:T(8,128)(2,1)} %constant.73.clone.refs_1_.refs_2_, bf16[512,512]{1,0:T(8,128)(2,1)} %constant.74.clone.refs_2_.refs_3_, ...), custom_call_target="tpu_custom_call" | custom-call | tf_op jit(solution)/shard_map/pallas_call | solution.py:171
  46.4 0.0 all-to-all-done.refs_0_
  46.4 0.0 copy-start.1
  46.4 8.6 %all-to-all-start.1 = ((f32[8,128,128]{2,1,0:T(8,128)}), f32[8,128,128]{2,1,0:T(8,128)S(1)}, u32[]{:S(2)}, u32[]{:S(2)}) async-start(f32[8,128,128]{2,1,0:T(8,128)} %bitcast.17), calls=%async_computation.1 | async-start | bytes 1048576 | tf_op jit(solution)/shard_map/all_to_all | solution.py:336
  55.0 0.7 multiply_reduce_fusion
  55.7 0.1 mul.24
  55.8 0.7 reshape.23.taps_ref
  56.5 4.4 %table.1 = (bf16[512,2048]{1,0:T(8,128)(2,1)}, bf16[512,2048]{1,0:T(8,128)(2,1)}) custom-call(f32[2,256,128]{2,1,0:T(8,128)} %constant.78.clone.base_ref, f32[2,256,8]{2,1,0:T(8,128)} %constant.79.clone.turn_ref), custom_call_target="tpu_custom_call" | custom-call | tf_op jit(solution)/shard_map/table/pallas_call | solution.py:215
  60.8 7.5 %all-to-all-done.1.refs_1_ = f32[8,128,128]{2,1,0:T(8,128)S(1)} async-done(((f32[8,128,128]{2,1,0:T(8,128)}), f32[8,128,128]{2,1,0:T(8,128)S(1)}, u32[]{:S(2)}, u32[]{:S(2)}) %all-to-all-start.1) | async-done | bytes 524320 | tf_op jit(solution)/shard_map/all_to_all | solution.py:336
  68.3 0.0 copy-start.2
  68.3 0.0 copy-done.1
  68.3 0.8 %copy-done.2 = f32[8,128,128]{2,1,0:T(8,128)} copy-done((f32[8,128,128]{2,1,0:T(8,128)}, f32[8,128,128]{2,1,0:T(8,128)S(1)}, u32[]{:S(2)}) %copy-start.2) | copy-done | bytes 524312
  69.1 8.1 %fine.1 = f32[2,4,1024,128]{3,2,1,0:T(8,128)} custom-call(f32[1,512]{1,0:T(1,128)} %reshape.23.taps_ref, f32[8,128,128]{2,1,0:T(8,128)} %copy-done.1, f32[8,128,128]{2,1,0:T(8,128)} %copy-done.2, bf16[512,2048]{1,0:T(8,128)(2,1)} %get-tuple-element.7.refs_2_, bf16[512,2048]{1,0:T(8,128)(2,1)} %get-tuple-element.8.refs_3_), custom_call_target="tpu_custom_call" | custom-call | tf_op jit(solution)/shard_map/fine/pallas_call | solution.py:265
  (3 shorter events, 0.0 us)
Async XLA Ops:
  0.0 17.1 %copy-start = (f32[2,1,32,4096]{3,2,1,0:T(8,128)S(1)}, f32[2,1,32,4096]{3,2,1,0:T(8,128)}, u32[]{:S(2)}) copy-start(f32[2,1,32,4096]{3,2,1,0:T(8,128)} %param.16) | copy-start | bytes 3145732
  9.9 36.5 %all-to-all-start = ((f32[8,128,128]{2,1,0:T(8,128)}), f32[8,128,128]{2,1,0:T(8,128)S(1)}, u32[]{:S(2)}, u32[]{:S(2)}) async-start(f32[8,128,128]{2,1,0:T(8,128)} %bitcast.18), calls=%async_computation | async-start | bytes 1048576 | tf_op jit(solution)/shard_map/all_to_all | solution.py:336
  17.2 19.9 %collective-permute-start = (f32[2,15,4096]{2,1,0:T(8,128)S(1)}, f32[2,15,4096]{2,1,0:T(8,128)S(1)}, u32[]{:S(2)}, u32[]{:S(2)}) collective-permute-start(f32[2,15,4096]{2,1,0:T(8,128)S(1)} %slice.8), channel_id=1, source_target_pairs={{2,0},{4,2},{6,4},{8,6},{10,8},{12,10},{14,12},{3,1},{5,3},{7,5},{... | collective-permute-start | bytes 1474568 | tf_op jit(solution)/shard_map/ppermute | solution.py:281
  37.1 0.8 %copy-start.3 = (f32[2,15,4096]{2,1,0:T(8,128)}, f32[2,15,4096]{2,1,0:T(8,128)S(1)}, u32[]{:S(2)}) copy-start(f32[2,15,4096]{2,1,0:T(8,128)S(1)} %collective-permute-done.refs_0_) | copy-start | bytes 1474564
  46.4 21.9 %copy-start.1 = (f32[8,128,128]{2,1,0:T(8,128)}, f32[8,128,128]{2,1,0:T(8,128)S(1)}, u32[]{:S(2)}) copy-start(f32[8,128,128]{2,1,0:T(8,128)S(1)} %all-to-all-done.refs_0_) | copy-start | bytes 1572868
  46.4 21.9 %all-to-all-start.1 = ((f32[8,128,128]{2,1,0:T(8,128)}), f32[8,128,128]{2,1,0:T(8,128)S(1)}, u32[]{:S(2)}, u32[]{:S(2)}) async-start(f32[8,128,128]{2,1,0:T(8,128)} %bitcast.17), calls=%async_computation.1 | async-start | bytes 1048576 | tf_op jit(solution)/shard_map/all_to_all | solution.py:336
  68.3 0.8 %copy-start.2 = (f32[8,128,128]{2,1,0:T(8,128)}, f32[8,128,128]{2,1,0:T(8,128)S(1)}, u32[]{:S(2)}) copy-start(f32[8,128,128]{2,1,0:T(8,128)S(1)} %all-to-all-done.1.refs_1_) | copy-start | bytes 1572868
